TPU v7x, 32 devices: a whole 2x2x4 slice. The times are simulated.
32 devices in a mesh: gx: 2 (over x), gy: 4 (over y, core), gz: 4 (over z).
Axes of the slice: x: 2, y: 2, z: 4, core: 2. Of those that a mesh axis runs over, the one named last changes fastest.
Arguments:
- features: bfloat16 [256, 4096], P('gz', ('gy', 'gx')), may hold values from -14 to 14, as said below
- tiles: bfloat16 [32, 32, 128, 128], P('gx', 'gy'), may hold values from -0.5 to 0.5
- block_mask: int32 [32, 32], P('gx', 'gy'), may hold values from 0 to 1, as said below
- tile_counts: int32 [32], P('gx'), may hold values from 1 to 32, as said below
- weight: bfloat16 [256, 256], replicated, may hold values from -0.375 to 0.375
- gamma: float32 [256], P('gz'), may hold values from 0.5 to 2
- beta: float32 [256], P('gz'), may hold values from -3 to 3
Outputs:
- normed: bfloat16 [256, 4096], P('gz', ('gx', 'gy'))
Inputs may be any that keep to these rules, and one draw needn't show every extreme that they name: `features`: channels along dimension 0, nodes along dimension 1. `block_mask`: 1 where block row and block column meet in a nonzero block, else 0; the diagonal is 1. tile_counts[r] is the number of ones in row r of block_mask.
All inputs are finite; a program needn't handle non-finite values.
Results may differ from a plain program's by a relative error of at most 0.013.
Values may be sent and summed in bfloat16 or wider, within the bound.
A program may use at most 64 MiB of HBM per device.

v0:
```python
import jax
import jax.numpy as jnp
from jax import lax
from jax.sharding import PartitionSpec as P


def body(features, tiles, block_mask, tile_counts, weight, gamma, beta):
    panel = lax.all_gather(features, "gx", axis=1, tiled=True)
    local_ch = panel.shape[0]
    rows_blk = tiles.shape[0]
    cols_blk = tiles.shape[1]
    tile_len = tiles.shape[2]
    panels = panel.reshape(local_ch, cols_blk, tile_len)
    prods = jnp.einsum("fcn,rcmn->frcm", panels, tiles, preferred_element_type=jnp.float32)
    share = block_mask.astype(jnp.float32) / tile_counts.astype(jnp.float32)[:, None]
    partial_value = jnp.einsum("frcm,rc->frm", prods, share).reshape(local_ch, rows_blk * tile_len)
    summed = lax.psum(partial_value, "gy")
    width = rows_blk * tile_len // lax.axis_size("gy")
    agg = lax.dynamic_slice_in_dim(summed, lax.axis_index("gy") * width, width, 1)
    agg = agg.astype(jnp.bfloat16)
    offset = lax.axis_index("gz") * local_ch
    full = lax.all_gather(agg, "gz", axis=0, tiled=True)
    w_cols = lax.dynamic_slice_in_dim(weight, offset, local_ch, 1)
    z_vals = jnp.einsum("co,cn->on", w_cols, full, preferred_element_type=jnp.float32)
    total = z_vals.shape[1] * lax.axis_size(("gx", "gy"))
    sums, squares = lax.psum(
        (jnp.sum(z_vals, axis=1), jnp.sum(z_vals * z_vals, axis=1)), ("gx", "gy")
    )
    mean = sums / total
    var = squares / total - mean * mean
    centered = z_vals - mean[:, None]
    scaled = gamma[:, None] * centered * lax.rsqrt(var + 1e-05)[:, None] + beta[:, None]
    return jnp.maximum(scaled, 0.0).astype(jnp.bfloat16)


def solution(mesh):
    in_specs = (
        P("gz", ("gy", "gx")),
        P("gx", "gy", None, None),
        P("gx", "gy"),
        P("gx"),
        P(),
        P("gz"),
        P("gz"),
    )
    out_specs = P("gz", ("gx", "gy"))
    return jax.shard_map(body, mesh=mesh, in_specs=in_specs, out_specs=out_specs, check_vma=False)
```

profile of v0, /device:TPU:0, one launch (start us, length us, event | category | flops | bytes accessed | tf_op | source)
XLA Modules:
  0.0 57.3 jit_solution(9171550169248883873)
XLA Ops:
  0.0 0.0 copy-start
  0.0 0.7 %convert_element_type.13 = f32[16]{0:T(128)S(1)} convert(s32[16]{0:T(128)} %param.10) | non-fusion elementwise | flops 16 | bytes 128 | tf_op jit(solution)/shard_map/convert_element_type | solution.py:15
  0.7 0.7 %divide_bitcast_fusion = bf16[16,8,1,1]{0,1,2,3:T(8,128)(2,1)S(1)} fusion(s32[16,8]{0,1:T(8,128)} %param.9, f32[16]{0:T(128)S(1)} %convert_element_type.13), kind=kLoop, calls=%fused_computation.12 | loop fusion | flops 384 | bytes 832 | tf_op jit(solution)/shard_map/div | solution.py:15
  1.4 0.1 copy.12
  1.5 6.1 %all_gather.6 = bf16[64,1024]{1,0:T(8,128)(2,1)S(1)} all-gather(bf16[64,512]{1,0:T(8,128)(2,1)} %param.7), channel_id=1, replica_groups=mesh['gx'=2,'gy'=4,'gz'=4] {'gx'}, dimensions={1}, use_global_device_ids=true | all-gather | bytes 196608 | tf_op jit(solution)/shard_map/all_gather | solution.py:8
  7.6 3.8 %fusion.4 = bf16[64,16,8,128]{3,0,1,2:T(8,128)(2,1)S(1)} fusion(bf16[16,8,128,128]{3,2,1,0:T(8,128)(2,1)} %param.8, bf16[64,8,128,1]{2,1,0,3:T(8,128)(2,1)S(1)} %bitcast.19), kind=kOutput, calls=%fused_computation.4 | convolution fusion | flops 268435456 | bytes 6422528 | tf_op jit(solution)/shard_map/fcn,rcmn->frcm/dot_general | solution.py:14
  11.4 1.4 %fusion = f32[16,1,64,128]{3,1,2,0:T(1,128)S(1)} fusion(bf16[16,8,1,1]{1,2,3,0:T(2,128)(2,1)S(1)} %copy.12, bf16[64,16,8,128]{3,0,1,2:T(8,128)(2,1)S(1)} %fusion.4), kind=kOutput, calls=%fused_computation | convolution fusion | flops 2097152 | bytes 2621696 | tf_op jit(solution)/shard_map/frcm,rc->frm/dot_general | solution.py:16
  12.8 0.0 copy-start.1
  12.8 0.0 copy-start.2
  12.8 0.3 copy.14
  13.2 0.2 copy.28
  13.3 16.7 %all-reduce.2 = bf16[64,2048]{1,0:T(8,128)(2,1)S(1)} all-reduce(f32[64,2048]{1,0:T(8,128)S(1)} %bitcast.18), channel_id=1, replica_groups=mesh['gx'=2,'gy'=4,'gz'=4] {'gy'}, use_global_device_ids=true, to_apply=%region_0.0 | all-reduce | flops 131072 | bytes 786432 | tf_op jit(solution)/shard_map/psum | solution.py:17
  30.1 14.2 %all_gather.7 = bf16[256,512]{1,0:T(8,128)(2,1)S(1)} all-gather(bf16[64,512]{1,0:T(8,128)(2,1)S(1)} %dynamic-slice_convert_fusion), channel_id=1, replica_groups=mesh['gx'=2,'gy'=4,'gz'=4] {'gz'}, dimensions={0}, use_global_device_ids=true | all-gather | bytes 327680 | tf_op jit(solution)/shard_map/all_gather | solution.py:22
  44.3 0.0 copy-done
  44.3 0.4 fusion.11
  44.7 11.8 %all-reduce = (f32[64]{0:T(128)S(1)}, f32[64]{0:T(128)S(1)}) all-reduce(f32[64]{0:T(128)S(1)} %get-tuple-element.6, f32[64]{0:T(128)S(1)} %get-tuple-element.5), channel_id=1, replica_groups=mesh['gx'=2,'gy'=4,'gz'=4] {'gx','gy'}, use_global_device_ids=true, to_apply=%region_4.0 | all-reduce | flops 128 | bytes 1024 | tf_op jit(solution)/shard_map/psum | solution.py:26
  56.5 0.0 copy-done.1
  56.5 0.0 copy-done.2
  56.5 0.7 %maximum_convert_fusion = bf16[64,512]{1,0:T(8,128)(2,1)} fusion(f32[64,512]{1,0:T(8,128)S(1)} %get-tuple-element.11, f32[64]{0:T(128)S(1)} %copy-done.1, f32[64]{0:T(128)S(1)} %get-tuple-element.10, f32[64]{0:T(128)S(1)} %get-tuple-element.9, f32[64]{0:T(128)S(1)} %copy-done.2), kind=kLoop, calls=%fused_computation.7 | loop fusion | flops 196608 | bytes 197632 | tf_op jit(solution)/shard_map/convert_element_type | solution.py:33
  (3 shorter events, 0.0 us)
Async XLA Ops:
  0.0 44.3 %copy-start = (bf16[256,256]{1,0:T(8,128)(2,1)S(1)}, bf16[256,256]{1,0:T(8,128)(2,1)}, u32[]{:S(2)}) copy-start(bf16[256,256]{1,0:T(8,128)(2,1)} %param.11) | copy-start | bytes 393220
  12.8 43.7 %copy-start.1 = (f32[64]{0:T(128)S(1)}, f32[64]{0:T(128)}, u32[]{:S(2)}) copy-start(f32[64]{0:T(128)} %param.13) | copy-start | bytes 772
  12.8 43.7 %copy-start.2 = (f32[64]{0:T(128)S(1)}, f32[64]{0:T(128)}, u32[]{:S(2)}) copy-start(f32[64]{0:T(128)} %param.12) | copy-start | bytes 772
where the time goes:
time: 57.5 us; the launch traced here: 57.3 us
  blocking collectives  48.9 us (85%)
  matrix products  5.54 us (10%)
  other arithmetic  2.13 us (4%)
  local copies, waits for them, and re-layouts  0.61 us (1%)
    psum x1, blocking collectives, body(): summed = lax.psum(partial_value, 'gy')  16.7 us
    all_gather x1, blocking collectives, body(): full = lax.all_gather(agg, 'gz', axis=0, tiled=True)  14.2 us
    psum x1, blocking collectives, body(): lax.psum((jnp.sum(z_vals, axis=1), jnp.sum(z_vals * z_vals, axis=1)), ('g...  11.8 us
    all_gather x1, blocking collectives, body(): panel = lax.all_gather(features, 'gx', axis=1, tiled=True)  6.13 us
    dot_general x1, matrix products, body(): jnp.einsum('fcn,rcmn->frcm', panels, tiles, preferred_element_type=jnp.fl...  3.75 us
    dot_general x1, matrix products, body(): jnp.einsum('frcm,rc->frm', prods, share)  1.42 us

commit v1 on v0

v1 whole, which is shorter than its diff:
```python
import functools

import jax
import jax.numpy as jnp
from jax import lax
from jax.experimental import pallas as pl
from jax.experimental.pallas import tpu as pltpu
from jax.sharding import PartitionSpec as P

MESH = pl.DeviceIdType.MESH
CHUNKS = 2


def kernel(
    sizes, chunks,
    feat_hbm, tiles_hbm, mask_ref, count_ref, weight_hbm, gamma_hbm, beta_hbm,
    out_ref,
    panel, tiles, weight, w_rows, gamma, beta, acc, mine, part_out, part_in, full, z_scr,
    stat_out, stat_in,
    load_sem, tile_sem, x_send, x_recv, y_send, y_recv, z_send, z_recv, s_send, s_recv,
):
    nx, ny, nz = sizes
    gx, gy, gz = lax.axis_index("gx"), lax.axis_index("gy"), lax.axis_index("gz")
    rows_blk, cols_blk, tile_len, _ = tiles.shape
    local_ch = panel.shape[1]
    cpl = cols_blk // nx
    rpd = rows_blk // ny
    rc = rpd // chunks
    span = rc * tile_len
    f32, bf16 = jnp.float32, jnp.bfloat16

    loads = [
        pltpu.make_async_copy(feat_hbm, panel.at[gx], load_sem.at[0]),
        pltpu.make_async_copy(weight_hbm, weight, load_sem.at[1]),
        pltpu.make_async_copy(gamma_hbm, gamma, load_sem.at[2]),
        pltpu.make_async_copy(beta_hbm, beta, load_sem.at[3]),
    ]
    loads[0].start()
    tile_loads = {}
    for s in range(nx):
        col = lax.rem(gx + s, nx) * cpl
        for g in range(ny):
            tile_loads[s, g] = pltpu.make_async_copy(
                tiles_hbm.at[pl.ds(g * rpd, rpd), pl.ds(col, cpl)],
                tiles.at[pl.ds(g * rpd, rpd), pl.ds(col, cpl)],
                tile_sem.at[s, g],
            )

    barrier = pltpu.get_barrier_semaphore()
    xy_peers = [
        (lax.rem(gx + i, nx), lax.rem(gy + j, ny), gz)
        for i in range(nx) for j in range(ny) if i or j
    ]
    z_peers = [(gx, gy, lax.rem(gz + k, nz)) for k in range(1, nz)]
    for peer in xy_peers + z_peers:
        pl.semaphore_signal(barrier, inc=1, device_id=peer, device_id_type=MESH)
    for g in range(ny):
        tile_loads[0, g].start()
    for load in loads[1:]:
        load.start()
    for s in range(1, nx):
        for g in range(ny):
            tile_loads[s, g].start()
    loads[0].wait()
    pl.semaphore_wait(barrier, len(xy_peers) + len(z_peers))

    x_copies = []
    for s in range(1, nx):
        copy = pltpu.make_async_remote_copy(
            src_ref=panel.at[gx], dst_ref=panel.at[gx],
            send_sem=x_send.at[s - 1], recv_sem=x_recv.at[s - 1],
            device_id=(lax.rem(gx + s, nx), gy, gz), device_id_type=MESH,
        )
        copy.start()
        x_copies.append(copy)

    loads[1].wait()
    w_rows[...] = weight[...].T
    for load in loads[2:]:
        load.wait()

    def product(r, src):
        lhs, rhs = [], []
        for j in range(cpl):
            flag = mask_ref[r, src * cpl + j].astype(f32)
            block = panel[src, :, j * tile_len:(j + 1) * tile_len]
            lhs.append(block * jnp.full(block.shape, flag, f32).astype(bf16))
            rhs.append(tiles[r, src * cpl + j])
        return lax.dot_general(
            jnp.concatenate(lhs, axis=1), jnp.concatenate(rhs, axis=1),
            (((1,), (1,)), ((), ())), preferred_element_type=f32,
        )

    for g in range(ny):
        tile_loads[0, g].wait()
        for i in range(rpd):
            acc[g * rpd + i] = product(g * rpd + i, gx)
    for s in range(1, nx):
        for g in range(ny):
            tile_loads[s, g].wait()
        src = lax.rem(gx + nx - s, nx)
        x_copies[s - 1].wait()
        if s < nx - 1:
            for r in range(rows_blk):
                acc[r] += product(r, src)
    last = lax.rem(gx + 1, nx)

    y_copies = {}
    for h in range(chunks):
        for k in list(range(1, ny)) + [0]:
            dest = lax.rem(gy + k, ny)
            for i in range(rc):
                r = dest * rpd + h * rc + i
                total = acc[r]
                if nx > 1:
                    total = total + product(r, last)
                count = jnp.full(total.shape, count_ref[r].astype(f32), f32)
                total = total / count
                cols = slice(i * tile_len, (i + 1) * tile_len)
                if k:
                    part_out[k - 1, h, :, cols] = total.astype(bf16)
                else:
                    mine[h, :, cols] = total
            if k:
                copy = pltpu.make_async_remote_copy(
                    src_ref=part_out.at[k - 1, h], dst_ref=part_in.at[k - 1, h],
                    send_sem=y_send.at[k - 1, h], recv_sem=y_recv.at[k - 1, h],
                    device_id=(gx, dest, gz), device_id_type=MESH,
                )
                copy.start()
                y_copies[k, h] = copy

    z_copies = {}
    ch = pl.ds(pl.multiple_of(gz * local_ch, local_ch), local_ch)
    for h in range(chunks):
        total = mine[h]
        for k in range(1, ny):
            y_copies[k, h].wait_recv()
            total = total + part_in[k - 1, h].astype(f32)
        full[h, ch, :] = total.astype(bf16)
        for k in range(1, nz):
            copy = pltpu.make_async_remote_copy(
                src_ref=full.at[h, ch], dst_ref=full.at[h, ch],
                send_sem=z_send.at[k - 1, h], recv_sem=z_recv.at[k - 1, h],
                device_id=z_peers[k - 1], device_id_type=MESH,
            )
            copy.start()
            z_copies[k, h] = copy

    w_local = w_rows[ch, :]
    sums = jnp.zeros((local_ch, 1), f32)
    squares = jnp.zeros((local_ch, 1), f32)
    for h in range(chunks):
        for k in range(1, nz):
            z_copies[k, h].wait_recv()
        z_vals = jnp.dot(w_local, full[h], preferred_element_type=f32)
        z_scr[h] = z_vals
        sums += jnp.sum(z_vals, axis=1, keepdims=True)
        squares += jnp.sum(z_vals * z_vals, axis=1, keepdims=True)
    lane = lax.broadcasted_iota(jnp.int32, (local_ch, 128), 1)
    stacked = jnp.where(lane == 0, sums, jnp.where(lane == 1, squares, 0.0))
    stat_out[...] = stacked.T[0:8, :]
    s_copies = []
    for k, peer in enumerate(xy_peers):
        copy = pltpu.make_async_remote_copy(
            src_ref=stat_out, dst_ref=stat_in.at[k],
            send_sem=s_send.at[k], recv_sem=s_recv.at[k],
            device_id=peer, device_id_type=MESH,
        )
        copy.start()
        s_copies.append(copy)
    stats = stat_out[...]
    for k, copy in enumerate(s_copies):
        copy.wait_recv()
        stats = stats + stat_in[k]
    nodes = span * chunks * nx * ny
    mean = stats[0:1, :] / nodes
    var = stats[1:2, :] / nodes - mean * mean
    scale = gamma[...] * lax.rsqrt(var + 1e-05)
    row = lax.broadcasted_iota(jnp.int32, (8, local_ch), 0)
    table = jnp.where(row == 0, mean, jnp.where(row == 1, scale, beta[...]))
    cols = table.T
    mean_c, scale_c, beta_c = cols[:, 0:1], cols[:, 1:2], cols[:, 2:3]
    for h in range(chunks):
        value = (z_scr[h] - mean_c) * scale_c + beta_c
        out_ref[:, h * span:(h + 1) * span] = jnp.maximum(value, 0.0).astype(bf16)

    for copy in list(y_copies.values()) + list(z_copies.values()) + s_copies:
        copy.wait_send()


def body(sizes, features, tiles, block_mask, tile_counts, weight, gamma, beta):
    nx, ny, nz = sizes
    local_ch, nodes = features.shape
    rows_blk, cols_blk, tile_len, _ = tiles.shape
    width = rows_blk * tile_len // ny
    rpd = rows_blk // ny
    chunks = CHUNKS if rpd % CHUNKS == 0 else 1
    span = width // chunks
    f32, bf16 = jnp.float32, jnp.bfloat16
    peers = nx * ny - 1
    dma = pltpu.SemaphoreType.DMA
    hbm = pl.BlockSpec(memory_space=pl.ANY)
    smem = pl.BlockSpec(memory_space=pltpu.SMEM)
    return pl.pallas_call(
        functools.partial(kernel, sizes, chunks),
        out_shape=jax.ShapeDtypeStruct((local_ch, width), bf16),
        in_specs=[hbm, hbm, smem, smem, hbm, hbm, hbm],
        out_specs=pl.BlockSpec(memory_space=pltpu.VMEM),
        scratch_shapes=[
            pltpu.VMEM((nx, local_ch, nodes), bf16),
            pltpu.VMEM(tiles.shape, bf16),
            pltpu.VMEM(weight.shape, bf16),
            pltpu.VMEM(weight.shape[::-1], bf16),
            pltpu.VMEM((1, local_ch), f32),
            pltpu.VMEM((1, local_ch), f32),
            pltpu.VMEM((rows_blk, local_ch, tile_len), f32),
            pltpu.VMEM((chunks, local_ch, span), f32),
            pltpu.VMEM((max(ny - 1, 1), chunks, local_ch, span), bf16),
            pltpu.VMEM((max(ny - 1, 1), chunks, local_ch, span), bf16),
            pltpu.VMEM((chunks, local_ch * nz, span), bf16),
            pltpu.VMEM((chunks, local_ch, span), f32),
            pltpu.VMEM((8, local_ch), f32),
            pltpu.VMEM((max(peers, 1), 8, local_ch), f32),
            dma((4,)),
            dma((nx, ny)),
            dma((max(nx - 1, 1),)),
            dma((max(nx - 1, 1),)),
            dma((max(ny - 1, 1), chunks)),
            dma((max(ny - 1, 1), chunks)),
            dma((max(nz - 1, 1), chunks)),
            dma((max(nz - 1, 1), chunks)),
            dma((max(peers, 1),)),
            dma((max(peers, 1),)),
        ],
        compiler_params=pltpu.CompilerParams(collective_id=0, has_side_effects=True),
        name="graph_conv",
    )(features, tiles, block_mask, tile_counts, weight,
      gamma.reshape(1, local_ch), beta.reshape(1, local_ch))


def solution(mesh):
    in_specs = (
        P("gz", ("gy", "gx")),
        P("gx", "gy", None, None),
        P("gx", "gy"),
        P("gx"),
        P(),
        P("gz"),
        P("gz"),
    )
    out_specs = P("gz", ("gx", "gy"))
    sizes = tuple(mesh.shape[name] for name in ("gx", "gy", "gz"))
    return jax.shard_map(
        functools.partial(body, sizes), mesh=mesh, in_specs=in_specs,
        out_specs=out_specs, check_vma=False,
    )
```

time: 57.5 us -> 28.3 us (0.49)
  blocking collectives: 48.9 us -> 0 us
  Pallas kernels: 0 us -> 25.2 us
  matrix products: 5.54 us -> 0 us
  local copies, waits for them, and re-layouts: 0.61 us -> 2.83 us
  other arithmetic: 2.13 us -> 0 us
    psum x2 -> x0, blocking collectives: 28.6 us -> none  [the longest x1 16.7 us: body(): summed = lax.psum(partial_value, 'gy')]
    pallas_call x0 -> x1, Pallas kernels: none -> 25.2 us  [body(): pl.pallas_call(functools.partial(kernel, sizes, chunks), out_shape=jax.Sh...]
    all_gather x2 -> x0, blocking collectives: 20.4 us -> none  [the longest x1 14.2 us: body(): full = lax.all_gather(agg, 'gz', axis=0, tiled=True)]
    dot_general x3 -> x0, matrix products: 5.54 us -> none  [the longest x1 3.75 us: body(): jnp.einsum('fcn,rcmn->frcm', panels, tiles, preferred_element_type=jnp.fl...]
    unnamed x8 -> x2, local copies, waits for them, and re-layouts: 0.2 us -> 2.83 us
    convert_element_type x2 -> x0, other arithmetic: 1.43 us -> none  [the longest x1 0.74 us: body(): return jnp.maximum(scaled, 0.0).astype(jnp.bfloat16)]
    div x2 -> x0, other arithmetic: 0.7 us -> none  [the longest x1 0.69 us: body(): block_mask.astype(jnp.float32) / tile_counts.astype(jnp.float32)[:, None]]
where the time goes in v1:
time: 28.3 us; the launch traced here: 28.1 us
  Pallas kernels  25.2 us (89%)
  local copies, waits for them, and re-layouts  2.83 us (10%)
    pallas_call x1, Pallas kernels, body(): pl.pallas_call(functools.partial(kernel, sizes, chunks), out_shape=jax.Sh...  25.2 us
    unnamed x2, local copies, waits for them, and re-layouts  2.83 us

profile of v1, /device:TPU:0, one launch (start us, length us, event | category | flops | bytes accessed | tf_op | source)
XLA Modules:
  0.0 28.1 jit_solution(1397972184390366049)
XLA Ops:
  0.0 1.4 %copy.8.mask_ref = s32[16,8]{1,0:T(8,128)} copy(s32[16,8]{0,1:T(8,128)} %param.9) | data formatting | bytes 1024 | tf_op args[2]
  1.4 25.2 %graph_conv.1 = bf16[64,512]{1,0:T(8,128)(2,1)} custom-call(bf16[64,512]{1,0:T(8,128)(2,1)} %feat_hbm.1, bf16[16,8,128,128]{3,2,1,0:T(8,128)(2,1)} %tiles_hbm.1, s32[16,8]{1,0:T(8,128)} %copy.8.mask_ref, s32[16]{0:T(128)} %count_ref.1, bf16[256,256]{1,0:T(8,128)(2,1)} %weight_hbm.1, f32[1,64]{1,0:T(1,128)} %bitcast.2, f32[1,64]{1,0:T(1,128)} %bitcast.3), custom_call_target="tpu_custom_call" | custom-call | tf_op jit(solution)/shard_map/graph_conv/pallas_call | solution.py:205
  26.6 1.5 %copy.10 = bf16[64,512]{1,0:T(8,128)(2,1)} copy(bf16[64,512]{1,0:T(8,128)(2,1)} %graph_conv.1) | data formatting | bytes 131072

commit v2 on v1

--- a/solution.py
+++ b/solution.py
@@ -13,11 +13,11 @@
 
 def kernel(
     sizes, chunks,
-    feat_hbm, tiles_hbm, mask_ref, count_ref, weight_hbm, gamma_hbm, beta_hbm,
+    feat_hbm, tiles_hbm, mask_hbm, count_hbm, weight_hbm, gamma_hbm, beta_hbm,
     out_ref,
-    panel, tiles, weight, w_rows, gamma, beta, acc, mine, part_out, part_in, full, z_scr,
+    mask_ref, count_ref, panel, tiles, weight, w_rows, gamma, beta, acc, mine, part_out, part_in, full, z_scr,
     stat_out, stat_in,
-    load_sem, tile_sem, x_send, x_recv, y_send, y_recv, z_send, z_recv, s_send, s_recv,
+    load_sem, tile_sem, up_sem, down_sem, x_send, x_recv, y_send, y_recv, z_send, z_recv, s_send, s_recv,
 ):
     nx, ny, nz = sizes
     gx, gy, gz = lax.axis_index("gx"), lax.axis_index("gy"), lax.axis_index("gz")
@@ -34,8 +34,9 @@
         pltpu.make_async_copy(weight_hbm, weight, load_sem.at[1]),
         pltpu.make_async_copy(gamma_hbm, gamma, load_sem.at[2]),
         pltpu.make_async_copy(beta_hbm, beta, load_sem.at[3]),
+        pltpu.make_async_copy(mask_hbm, mask_ref, load_sem.at[4]),
+        pltpu.make_async_copy(count_hbm, count_ref, load_sem.at[5]),
     ]
-    loads[0].start()
     tile_loads = {}
     for s in range(nx):
         col = lax.rem(gx + s, nx) * cpl
@@ -47,13 +48,23 @@
             )
 
     barrier = pltpu.get_barrier_semaphore()
+    x_peers = [(lax.rem(gx + i, nx), gy, gz) for i in range(1, nx)]
+    y_peers = [(gx, lax.rem(gy + j, ny), gz) for j in range(1, ny)]
+    z_peers = [(gx, gy, lax.rem(gz + k, nz)) for k in range(1, nz)]
     xy_peers = [
         (lax.rem(gx + i, nx), lax.rem(gy + j, ny), gz)
         for i in range(nx) for j in range(ny) if i or j
     ]
-    z_peers = [(gx, gy, lax.rem(gz + k, nz)) for k in range(1, nz)]
-    for peer in xy_peers + z_peers:
-        pl.semaphore_signal(barrier, inc=1, device_id=peer, device_id_type=MESH)
+    above, below = (gx, gy, gz + 1), (gx, gy, gz - 1)
+
+    def signal(sem, peer):
+        pl.semaphore_signal(sem, inc=1, device_id=peer, device_id_type=MESH)
+
+    for peer in x_peers + y_peers:
+        signal(barrier, peer)
+    pl.when(gz < nz - 1)(lambda: signal(barrier, above))
+    pl.when(gz > 0)(lambda: signal(barrier, below))
+    loads[0].start()
     for g in range(ny):
         tile_loads[0, g].start()
     for load in loads[1:]:
@@ -62,7 +73,8 @@
         for g in range(ny):
             tile_loads[s, g].start()
     loads[0].wait()
-    pl.semaphore_wait(barrier, len(xy_peers) + len(z_peers))
+    z_near = (gz < nz - 1).astype(jnp.int32) + (gz > 0).astype(jnp.int32)
+    pl.semaphore_wait(barrier, len(x_peers) + len(y_peers) + z_near)
 
     x_copies = []
     for s in range(1, nx):
@@ -74,6 +86,9 @@
         copy.start()
         x_copies.append(copy)
 
+    pl.when((gz == 1) & (gz < nz - 1))(lambda: signal(up_sem, above))
+    pl.when((gz == nz - 2) & (gz > 0))(lambda: signal(down_sem, below))
+
     loads[1].wait()
     w_rows[...] = weight[...].T
     for load in loads[2:]:
@@ -82,7 +97,7 @@
     def product(r, src):
         lhs, rhs = [], []
         for j in range(cpl):
-            flag = mask_ref[r, src * cpl + j].astype(f32)
+            flag = mask_ref[src * cpl + j, r].astype(f32)
             block = panel[src, :, j * tile_len:(j + 1) * tile_len]
             lhs.append(block * jnp.full(block.shape, flag, f32).astype(bf16))
             rhs.append(tiles[r, src * cpl + j])
@@ -95,6 +110,17 @@
         tile_loads[0, g].wait()
         for i in range(rpd):
             acc[g * rpd + i] = product(g * rpd + i, gx)
+
+    @pl.when(gz > 1)
+    def _():
+        pl.semaphore_wait(up_sem, 1)
+        pl.when(gz < nz - 1)(lambda: signal(up_sem, above))
+
+    @pl.when(gz < nz - 2)
+    def _():
+        pl.semaphore_wait(down_sem, 1)
+        pl.when(gz > 0)(lambda: signal(down_sem, below))
+
     for s in range(1, nx):
         for g in range(ny):
             tile_loads[s, g].wait()
@@ -114,8 +140,8 @@
                 total = acc[r]
                 if nx > 1:
                     total = total + product(r, last)
-                count = jnp.full(total.shape, count_ref[r].astype(f32), f32)
-                total = total / count
+                count = jnp.full((1, tile_len), count_ref[r].astype(f32), f32)
+                total = total * (1.0 / count)
                 cols = slice(i * tile_len, (i + 1) * tile_len)
                 if k:
                     part_out[k - 1, h, :, cols] = total.astype(bf16)
@@ -201,13 +227,14 @@
     peers = nx * ny - 1
     dma = pltpu.SemaphoreType.DMA
     hbm = pl.BlockSpec(memory_space=pl.ANY)
-    smem = pl.BlockSpec(memory_space=pltpu.SMEM)
     return pl.pallas_call(
         functools.partial(kernel, sizes, chunks),
-        out_shape=jax.ShapeDtypeStruct((local_ch, width), bf16),
-        in_specs=[hbm, hbm, smem, smem, hbm, hbm, hbm],
+        out_shape=pltpu.VMEM((local_ch, width), bf16),
+        in_specs=[hbm] * 7,
         out_specs=pl.BlockSpec(memory_space=pltpu.VMEM),
         scratch_shapes=[
+            pltpu.SMEM((cols_blk, rows_blk), jnp.int32),
+            pltpu.SMEM((rows_blk,), jnp.int32),
             pltpu.VMEM((nx, local_ch, nodes), bf16),
             pltpu.VMEM(tiles.shape, bf16),
             pltpu.VMEM(weight.shape, bf16),
@@ -222,8 +249,10 @@
             pltpu.VMEM((chunks, local_ch, span), f32),
             pltpu.VMEM((8, local_ch), f32),
             pltpu.VMEM((max(peers, 1), 8, local_ch), f32),
-            dma((4,)),
+            dma((6,)),
             dma((nx, ny)),
+            pltpu.SemaphoreType.REGULAR,
+            pltpu.SemaphoreType.REGULAR,
             dma((max(nx - 1, 1),)),
             dma((max(nx - 1, 1),)),
             dma((max(ny - 1, 1), chunks)),
@@ -235,7 +264,7 @@
         ],
         compiler_params=pltpu.CompilerParams(collective_id=0, has_side_effects=True),
         name="graph_conv",
-    )(features, tiles, block_mask, tile_counts, weight,
+    )(features, tiles, block_mask.T, tile_counts, weight,
       gamma.reshape(1, local_ch), beta.reshape(1, local_ch))
 
 

time: 28.3 us -> 23.6 us (0.83)
  Pallas kernels: 25.2 us -> 22.8 us
  local copies, waits for them, and re-layouts: 2.83 us -> 0.63 us
    pallas_call x1, Pallas kernels: 25.2 us -> 22.8 us  [body(): pl.pallas_call(functools.partial(kernel, sizes, chunks), out_shape=pltpu....]
    unnamed x2 -> x1, local copies, waits for them, and re-layouts: 2.83 us -> 0.63 us
where the time goes in v2:
time: 23.6 us; the launch traced here: 23.4 us
  Pallas kernels  22.8 us (97%)
  local copies, waits for them, and re-layouts  0.63 us (3%)
    pallas_call x1, Pallas kernels, body(): pl.pallas_call(functools.partial(kernel, sizes, chunks), out_shape=pltpu....  22.8 us
    unnamed x1, local copies, waits for them, and re-layouts  0.63 us

profile of v2, /device:TPU:0, one launch (start us, length us, event | category | flops | bytes accessed | tf_op | source)
XLA Modules:
  0.0 23.4 jit_solution(1069361217528731445)
XLA Ops:
  0.0 22.8 %graph_conv.1 = bf16[64,512]{1,0:T(8,128)(2,1)S(1)} custom-call(bf16[64,512]{1,0:T(8,128)(2,1)} %feat_hbm.1, bf16[16,8,128,128]{3,2,1,0:T(8,128)(2,1)} %tiles_hbm.1, s32[8,16]{1,0:T(8,128)} %bitcast.3, s32[16]{0:T(128)} %count_hbm.1, bf16[256,256]{1,0:T(8,128)(2,1)} %weight_hbm.1, f32[1,64]{1,0:T(1,128)} %bitcast.4, f32[1,64]{1,0:T(1,128)} %bitcast.5), custom_call_target="tpu_custom_call" | custom-call | tf_op jit(solution)/shard_map/graph_conv/pallas_call | solution.py:230
  22.8 0.6 %copy.9 = bf16[64,512]{1,0:T(8,128)(2,1)} copy(bf16[64,512]{1,0:T(8,128)(2,1)S(1)} %graph_conv.1) | data formatting | bytes 131072

commit v3 on v2

--- a/solution.py
+++ b/solution.py
@@ -16,8 +16,8 @@
     feat_hbm, tiles_hbm, mask_hbm, count_hbm, weight_hbm, gamma_hbm, beta_hbm,
     out_ref,
     mask_ref, count_ref, panel, tiles, weight, w_rows, gamma, beta, acc, mine, part_out, part_in, full, z_scr,
-    stat_out, stat_in,
-    load_sem, tile_sem, up_sem, down_sem, x_send, x_recv, y_send, y_recv, z_send, z_recv, s_send, s_recv,
+    edge_out, edge_in, stat_out, stat_in, stat_sum,
+    load_sem, tile_sem, up_sem, down_sem, x_send, x_recv, y_send, y_recv, z_send, z_recv, e_send, e_recv, s_send, s_recv,
 ):
     nx, ny, nz = sizes
     gx, gy, gz = lax.axis_index("gx"), lax.axis_index("gy"), lax.axis_index("gz")
@@ -50,7 +50,6 @@
     barrier = pltpu.get_barrier_semaphore()
     x_peers = [(lax.rem(gx + i, nx), gy, gz) for i in range(1, nx)]
     y_peers = [(gx, lax.rem(gy + j, ny), gz) for j in range(1, ny)]
-    z_peers = [(gx, gy, lax.rem(gz + k, nz)) for k in range(1, nz)]
     xy_peers = [
         (lax.rem(gx + i, nx), lax.rem(gy + j, ny), gz)
         for i in range(nx) for j in range(ny) if i or j
@@ -156,63 +155,153 @@
                 copy.start()
                 y_copies[k, h] = copy
 
-    z_copies = {}
     ch = pl.ds(pl.multiple_of(gz * local_ch, local_ch), local_ch)
+    hubs = nz == 4
+    first = jnp.where(gz < 2, 2, 1)
+    edge = jnp.where(gz == 1, 0, nz - 1)
+    is_hub = (gz == 1) | (gz == 2)
+
+    def row_copy(h, slot, source, dest):
+        rows = pl.ds(pl.multiple_of(source * local_ch, local_ch), local_ch)
+        return pltpu.make_async_remote_copy(
+            src_ref=full.at[h, rows], dst_ref=full.at[h, rows],
+            send_sem=z_send.at[slot, h], recv_sem=z_recv.at[source, h],
+            device_id=(gx, gy, dest), device_id_type=MESH,
+        )
+
+    def gather_copies(h):
+        if hubs:
+            return [row_copy(h, 0, gz, first)], row_copy(h, 1, gz, 3 - first)
+        return [row_copy(h, k - 1, gz, lax.rem(gz + k, nz)) for k in range(1, nz)], None
+
     for h in range(chunks):
         total = mine[h]
         for k in range(1, ny):
             y_copies[k, h].wait_recv()
             total = total + part_in[k - 1, h].astype(f32)
         full[h, ch, :] = total.astype(bf16)
+        always, outer = gather_copies(h)
+        for copy in always:
+            copy.start()
+        if hubs:
+            pl.when(jnp.logical_not(is_hub))(outer.start)
+
+    def wait_rows(h):
         for k in range(1, nz):
-            copy = pltpu.make_async_remote_copy(
-                src_ref=full.at[h, ch], dst_ref=full.at[h, ch],
-                send_sem=z_send.at[k - 1, h], recv_sem=z_recv.at[k - 1, h],
-                device_id=z_peers[k - 1], device_id_type=MESH,
-            )
+            row_copy(h, 0, lax.rem(gz + k, nz), gz).wait_recv()
+
+    def channel_sums(vals):
+        return jnp.sum(vals, axis=1, keepdims=True), jnp.sum(vals * vals, axis=1, keepdims=True)
+
+    lane = lax.broadcasted_iota(jnp.int32, (local_ch, 128), 1)
+
+    def as_rows(columns):
+        stacked = jnp.zeros((local_ch, 128), f32)
+        for n, column in enumerate(columns):
+            stacked = jnp.where(lane == n, column, stacked)
+        return stacked.T[0:8, :]
+
+    npeer = len(xy_peers)
+
+    def stat_copy(which, k, peer):
+        return pltpu.make_async_remote_copy(
+            src_ref=stat_out.at[which], dst_ref=stat_in.at[k],
+            send_sem=s_send.at[which, k], recv_sem=s_recv.at[k],
+            device_id=peer, device_id_type=MESH,
+        )
+
+    def edge_copy(h, dest):
+        return pltpu.make_async_remote_copy(
+            src_ref=edge_out.at[h], dst_ref=edge_in.at[h],
+            send_sem=e_send.at[h], recv_sem=e_recv.at[h],
+            device_id=(gx, gy, dest), device_id_type=MESH,
+        )
+
+    own_stats = [stat_copy(0, k, peer) for k, peer in enumerate(xy_peers)]
+    edge_stats = [stat_copy(1, k, (peer[0], peer[1], edge)) for k, peer in enumerate(xy_peers)]
+    edge_stats.append(stat_copy(1, npeer, (gx, gy, edge)))
+
+    def whole_rows():
+        edge_ch = pl.ds(pl.multiple_of(edge * local_ch, local_ch), local_ch)
+        sums, squares, far_sums, far_squares, means = 0.0, 0.0, 0.0, 0.0, []
+        for h in range(chunks):
+            wait_rows(h)
+            if hubs:
+                z_far = jnp.dot(w_rows[edge_ch, :], full[h], preferred_element_type=f32)
+                s, q = channel_sums(z_far)
+                far_sums, far_squares = far_sums + s, far_squares + q
+                means.append(s / span)
+                edge_out[h] = (z_far - means[h]).astype(bf16)
+                edge_copy(h, edge).start()
+            if hubs and h == chunks - 1:
+                stat_out[1] = as_rows([far_sums, far_squares] + means)
+                for copy in edge_stats:
+                    copy.start()
+            z_vals = jnp.dot(w_rows[ch, :], full[h], preferred_element_type=f32)
+            z_scr[h] = z_vals
+            s, q = channel_sums(z_vals)
+            sums, squares = sums + s, squares + q
+        stat_out[0] = as_rows([sums, squares])
+        for copy in own_stats:
             copy.start()
-            z_copies[k, h] = copy
-
-    w_local = w_rows[ch, :]
-    sums = jnp.zeros((local_ch, 1), f32)
-    squares = jnp.zeros((local_ch, 1), f32)
-    for h in range(chunks):
-        for k in range(1, nz):
-            z_copies[k, h].wait_recv()
-        z_vals = jnp.dot(w_local, full[h], preferred_element_type=f32)
-        z_scr[h] = z_vals
-        sums += jnp.sum(z_vals, axis=1, keepdims=True)
-        squares += jnp.sum(z_vals * z_vals, axis=1, keepdims=True)
-    lane = lax.broadcasted_iota(jnp.int32, (local_ch, 128), 1)
-    stacked = jnp.where(lane == 0, sums, jnp.where(lane == 1, squares, 0.0))
-    stat_out[...] = stacked.T[0:8, :]
-    s_copies = []
-    for k, peer in enumerate(xy_peers):
-        copy = pltpu.make_async_remote_copy(
-            src_ref=stat_out, dst_ref=stat_in.at[k],
-            send_sem=s_send.at[k], recv_sem=s_recv.at[k],
-            device_id=peer, device_id_type=MESH,
-        )
-        copy.start()
-        s_copies.append(copy)
-    stats = stat_out[...]
-    for k, copy in enumerate(s_copies):
-        copy.wait_recv()
-        stats = stats + stat_in[k]
+        stats = stat_out[0]
+        for k, copy in enumerate(own_stats):
+            copy.wait_recv()
+            stats = stats + stat_in[k]
+        stat_sum[...] = stats
+
+    def edge_rows():
+        mine_rows = lax.broadcasted_iota(jnp.int32, (8, local_ch), 0) < 2
+        edge_stats[npeer].wait_recv()
+        stats = stat_in[npeer]
+        for k in range(npeer):
+            edge_stats[k].wait_recv()
+            stats = stats + jnp.where(mine_rows, stat_in[k], 0.0)
+        stat_sum[...] = stats
+        for h in range(chunks):
+            edge_copy(h, edge).wait_recv()
+            z_scr[h] = edge_in[h].astype(f32)
+
+    if hubs:
+        pl.when(is_hub)(whole_rows)
+        pl.when(jnp.logical_not(is_hub))(edge_rows)
+    else:
+        whole_rows()
+
     nodes = span * chunks * nx * ny
+    stats = stat_sum[...]
     mean = stats[0:1, :] / nodes
     var = stats[1:2, :] / nodes - mean * mean
     scale = gamma[...] * lax.rsqrt(var + 1e-05)
     row = lax.broadcasted_iota(jnp.int32, (8, local_ch), 0)
-    table = jnp.where(row == 0, mean, jnp.where(row == 1, scale, beta[...]))
+    table = jnp.where(row == 0, scale, jnp.where(row == 1, beta[...], stats - mean))
     cols = table.T
-    mean_c, scale_c, beta_c = cols[:, 0:1], cols[:, 1:2], cols[:, 2:3]
     for h in range(chunks):
-        value = (z_scr[h] - mean_c) * scale_c + beta_c
+        value = (z_scr[h] + cols[:, 2 + h:3 + h]) * cols[:, 0:1] + cols[:, 1:2]
         out_ref[:, h * span:(h + 1) * span] = jnp.maximum(value, 0.0).astype(bf16)
 
-    for copy in list(y_copies.values()) + list(z_copies.values()) + s_copies:
+    for copy in y_copies.values():
         copy.wait_send()
+    for h in range(chunks):
+        always, outer = gather_copies(h)
+        for copy in always:
+            copy.wait_send()
+        if hubs:
+            pl.when(jnp.logical_not(is_hub))(outer.wait_send)
+
+    def finish():
+        for copy in own_stats:
+            copy.wait_send()
+        if hubs:
+            for copy in edge_stats:
+                copy.wait_send()
+            for h in range(chunks):
+                edge_copy(h, edge).wait_send()
+
+    if hubs:
+        pl.when(is_hub)(finish)
+    else:
+        finish()
 
 
 def body(sizes, features, tiles, block_mask, tile_counts, weight, gamma, beta):
@@ -247,8 +336,11 @@
             pltpu.VMEM((max(ny - 1, 1), chunks, local_ch, span), bf16),
             pltpu.VMEM((chunks, local_ch * nz, span), bf16),
             pltpu.VMEM((chunks, local_ch, span), f32),
+            pltpu.VMEM((chunks, local_ch, span), bf16),
+            pltpu.VMEM((chunks, local_ch, span), bf16),
+            pltpu.VMEM((2, 8, local_ch), f32),
+            pltpu.VMEM((peers + 1, 8, local_ch), f32),
             pltpu.VMEM((8, local_ch), f32),
-            pltpu.VMEM((max(peers, 1), 8, local_ch), f32),
             dma((6,)),
             dma((nx, ny)),
             pltpu.SemaphoreType.REGULAR,
@@ -257,10 +349,12 @@
             dma((max(nx - 1, 1),)),
             dma((max(ny - 1, 1), chunks)),
             dma((max(ny - 1, 1), chunks)),
-            dma((max(nz - 1, 1), chunks)),
-            dma((max(nz - 1, 1), chunks)),
-            dma((max(peers, 1),)),
-            dma((max(peers, 1),)),
+            dma((max(nz - 1, 2), chunks)),
+            dma((nz, chunks)),
+            dma((chunks,)),
+            dma((chunks,)),
+            dma((2, peers + 1)),
+            dma((peers + 1,)),
         ],
         compiler_params=pltpu.CompilerParams(collective_id=0, has_side_effects=True),
         name="graph_conv",

time: 23.6 us -> 22.4 us (0.949)
  Pallas kernels: 22.8 us -> 21.6 us
    pallas_call x1, Pallas kernels: 22.8 us -> 21.6 us  [body(): pl.pallas_call(functools.partial(kernel, sizes, chunks), out_shape=pltpu....]
where the time goes in v3:
time: 22.4 us; the launch traced here: 22.3 us
  Pallas kernels  21.6 us (96%)
  local copies, waits for them, and re-layouts  0.63 us (3%)
    pallas_call x1, Pallas kernels, body(): pl.pallas_call(functools.partial(kernel, sizes, chunks), out_shape=pltpu....  21.6 us
    unnamed x1, local copies, waits for them, and re-layouts  0.63 us

profile of v3, /device:TPU:0, one launch (start us, length us, event | category | flops | bytes accessed | tf_op | source)
XLA Modules:
  0.0 22.3 jit_solution(16376480770011773175)
XLA Ops:
  0.0 21.6 %graph_conv.1 = bf16[64,512]{1,0:T(8,128)(2,1)S(1)} custom-call(bf16[64,512]{1,0:T(8,128)(2,1)} %feat_hbm.1, bf16[16,8,128,128]{3,2,1,0:T(8,128)(2,1)} %tiles_hbm.1, s32[8,16]{1,0:T(8,128)} %bitcast.3, s32[16]{0:T(128)} %count_hbm.1, bf16[256,256]{1,0:T(8,128)(2,1)} %weight_hbm.1, f32[1,64]{1,0:T(1,128)} %bitcast.4, f32[1,64]{1,0:T(1,128)} %bitcast.5), custom_call_target="tpu_custom_call" | custom-call | tf_op jit(solution)/shard_map/graph_conv/pallas_call | solution.py:319
  21.6 0.6 %copy.9 = bf16[64,512]{1,0:T(8,128)(2,1)} copy(bf16[64,512]{1,0:T(8,128)(2,1)S(1)} %graph_conv.1) | data formatting | bytes 131072

commit v4 on v3

--- a/solution.py
+++ b/solution.py
@@ -232,11 +232,13 @@
                 far_sums, far_squares = far_sums + s, far_squares + q
                 means.append(s / span)
                 edge_out[h] = (z_far - means[h]).astype(bf16)
+            if hubs and h < chunks - 1:
                 edge_copy(h, edge).start()
             if hubs and h == chunks - 1:
                 stat_out[1] = as_rows([far_sums, far_squares] + means)
                 for copy in edge_stats:
                     copy.start()
+                edge_copy(h, edge).start()
             z_vals = jnp.dot(w_rows[ch, :], full[h], preferred_element_type=f32)
             z_scr[h] = z_vals
             s, q = channel_sums(z_vals)

time: 22.4 us -> 22.1 us (0.987)
  Pallas kernels: 21.6 us -> 21.3 us
    pallas_call x1, Pallas kernels: 21.6 us -> 21.3 us  [body(): pl.pallas_call(functools.partial(kernel, sizes, chunks), out_shape=pltpu....]
where the time goes in v4:
time: 22.1 us; the launch traced here: 22 us
  Pallas kernels  21.3 us (96%)
  local copies, waits for them, and re-layouts  0.63 us (3%)
    pallas_call x1, Pallas kernels, body(): pl.pallas_call(functools.partial(kernel, sizes, chunks), out_shape=pltpu....  21.3 us
    unnamed x1, local copies, waits for them, and re-layouts  0.63 us

profile of v4, /device:TPU:0, one launch (start us, length us, event | category | flops | bytes accessed | tf_op | source)
XLA Modules:
  0.0 22.0 jit_solution(4719122984636288482)
XLA Ops:
  0.0 21.3 %graph_conv.1 = bf16[64,512]{1,0:T(8,128)(2,1)S(1)} custom-call(bf16[64,512]{1,0:T(8,128)(2,1)} %feat_hbm.1, bf16[16,8,128,128]{3,2,1,0:T(8,128)(2,1)} %tiles_hbm.1, s32[8,16]{1,0:T(8,128)} %bitcast.3, s32[16]{0:T(128)} %count_hbm.1, bf16[256,256]{1,0:T(8,128)(2,1)} %weight_hbm.1, f32[1,64]{1,0:T(1,128)} %bitcast.4, f32[1,64]{1,0:T(1,128)} %bitcast.5), custom_call_target="tpu_custom_call" | custom-call | tf_op jit(solution)/shard_map/graph_conv/pallas_call | solution.py:321
  21.3 0.6 %copy.9 = bf16[64,512]{1,0:T(8,128)(2,1)} copy(bf16[64,512]{1,0:T(8,128)(2,1)S(1)} %graph_conv.1) | data formatting | bytes 131072
